TPU v7x, 128 devices: a whole 4x4x4 slice. The times are simulated.
128 devices in a mesh: ctx: 16 (over x, z), head: 8 (over y, core).
Axes of the slice: x: 4, y: 4, z: 4, core: 2. Of those that a mesh axis runs over, the one named last changes fastest.
Arguments:
- input_x_channels: bfloat16 [16384, 8192], P('ctx', 'head'), may hold values from -4 to 4
- input_b_channels: bfloat16 [16384, 1024], P('ctx', 'head'), may hold values from -3 to 3
- input_c_channels: bfloat16 [16384, 1024], P('ctx', 'head'), may hold values from -3 to 3
- input_gate_channels: bfloat16 [16384, 8192], P('ctx', 'head'), may hold values from -75 to 75
- raw_step_sizes: float32 [128, 16384], P('head', 'ctx'), may hold values from -7 to 800
- log_decay_rate: float32 [128], P('head'), may hold values from -8 to -2.3
- head_skip_coeff: float32 [128], P('head'), may hold values from 0.5 to 2
- x_conv_taps: bfloat16 [4, 8192], P(None, 'head'), may hold values from -3 to 3
- b_conv_taps: bfloat16 [4, 1024], P(None, 'head'), may hold values from -3 to 3
- c_conv_taps: bfloat16 [4, 1024], P(None, 'head'), may hold values from -3 to 3
- gated_norm_gain: bfloat16 [8192], P('head'), may hold values from 0.099609375 to 1.8984375
- output_weight: bfloat16 [8192, 4096], P('head'), may hold values from -0.0625 to 0.0625
- adapter_down_panels: bfloat16 [96, 8192, 64], P('ctx', 'head'), may hold values from -0.0625 to 0.0625
- adapter_up_panels: bfloat16 [96, 64, 4096], P('ctx', None, 'head'), may hold values from -0.75 to 0.75
- turn_first_token: int32 [32], replicated, may hold values from 0 to 16256, as said below
- tenant_of_turn: int32 [32], replicated, may hold values from 0 to 95
- tenant_panel_index: int32 [96], replicated, may hold values from 0 to 95, each once
Outputs:
- out: bfloat16 [16384, 4096], P('ctx', 'head')
Inputs may be any that keep to these rules, and one draw needn't show every extreme that they name: `turn_first_token`: strictly increasing multiples of 128; the first is 0; every aligned block of 1024 tokens holds exactly 2 starts, and in every block but the first the earlier of them lies past the block's first token.
All inputs are finite; a program needn't handle non-finite values.
Results may differ from a plain program's by a relative error of at most 0.014.
Values may be sent and summed in bfloat16 or wider, within the bound.
A program may use at most 128 MiB of HBM per device.

v0:
```python
import jax
import jax.numpy as jnp
from jax import lax
from jax.sharding import PartitionSpec as P

P_SIZE = 64
N = 128
K = 4
Q = 128
TURN_DEV = 2
highest = lax.Precision.HIGHEST
epsilon = 1e-05


def shifted(block, axis, distance):
    devices = range(lax.axis_size(axis))
    route = [(i - distance, i) for i in devices if i - distance in devices]
    return lax.ppermute(block, axis, route)


def conv_rows(sequence, tail_rows, weight):
    token_rows = sequence.shape[0]
    joined = jnp.concatenate([tail_rows, sequence], axis=0).astype(jnp.float32)
    total = jnp.zeros((token_rows, sequence.shape[1]), jnp.float32)
    for tap in range(weight.shape[0]):
        total = total + weight[tap].astype(jnp.float32) * joined[tap : tap + token_rows]
    return jax.nn.silu(total).astype(jnp.bfloat16)


def local(
    input_x_channels,
    input_b_channels,
    input_c_channels,
    input_gate_channels,
    raw_step_sizes,
    log_decay_rate,
    head_skip_coeff,
    x_conv_taps,
    b_conv_taps,
    c_conv_taps,
    gated_norm_gain,
    output_weight,
    adapter_down_panels,
    adapter_up_panels,
    turn_first_token,
    tenant_of_turn,
    tenant_panel_index,
):
    token_rows = input_x_channels.shape[0]
    head_count = log_decay_rate.shape[0]
    group_count = input_b_channels.shape[1] // N
    per_group = head_count // group_count
    conv_edge = K - 1
    conv_tails = shifted(
        (
            input_x_channels[token_rows - conv_edge :],
            input_b_channels[token_rows - conv_edge :],
            input_c_channels[token_rows - conv_edge :],
        ),
        "ctx",
        1,
    )
    x_conv = conv_rows(input_x_channels, conv_tails[0], x_conv_taps)
    b_conv = conv_rows(input_b_channels, conv_tails[1], b_conv_taps)
    c_conv = conv_rows(input_c_channels, conv_tails[2], c_conv_taps)
    block_count = token_rows // Q
    step_sizes = jax.nn.softplus(raw_step_sizes)
    decay_rate = jnp.exp(log_decay_rate)
    step_heads = step_sizes.reshape(head_count, block_count, Q)
    running = jnp.cumsum(-step_heads * decay_rate[:, None, None], axis=2)
    run_blocks = running.transpose(1, 0, 2).reshape(block_count, group_count, per_group, Q)
    step_blocks = step_heads.transpose(1, 0, 2).reshape(block_count, group_count, per_group, Q)
    x_blocks = x_conv.astype(jnp.float32).reshape(block_count, Q, group_count, per_group, P_SIZE)
    b_blocks = b_conv.astype(jnp.float32).reshape(block_count, Q, group_count, N)
    c_blocks = c_conv.astype(jnp.float32).reshape(block_count, Q, group_count, N)
    scores = jnp.einsum("cqgn,ckgn->cgqk", c_blocks, b_blocks, precision=highest)
    causal = jnp.arange(Q)[:, None] >= jnp.arange(Q)[None, :]
    log_gap = run_blocks[..., :, None] - run_blocks[..., None, :]
    decay_mat = jnp.where(causal, jnp.exp(jnp.where(causal, log_gap, 0.0)), 0.0)
    mixing = scores[:, :, None] * decay_mat * step_blocks[..., None, :]
    y_local = jnp.einsum("cghqk,ckghp->cqghp", mixing, x_blocks, precision=highest)
    tail_weight = jnp.exp(run_blocks[..., -1:] - run_blocks) * step_blocks
    block_states = jnp.einsum(
        "cghk,ckghp,ckgn->cghpn", tail_weight, x_blocks, b_blocks, precision=highest
    )
    block_log = run_blocks[..., -1]

    def carry_step(carried, inputs):
        fresh_state, step_log = inputs
        return (jnp.exp(step_log)[..., None, None] * carried + fresh_state, carried)

    empty_state = jnp.zeros((group_count, per_group, P_SIZE, N), jnp.float32)
    device_state, before = lax.scan(carry_step, empty_state, (block_states, block_log))
    device_log = jnp.sum(block_log, axis=0)
    run_tokens = run_blocks.transpose(0, 3, 1, 2)
    y_local = y_local + jnp.exp(run_tokens)[..., None] * jnp.einsum(
        "cqgn,cghpn->cqghp", c_blocks, before, precision=highest
    )
    all_logs, states = (
        lax.all_gather(device_log[None], "ctx", axis=0, tiled=True),
        lax.all_gather(device_state[None], "ctx", axis=0, tiled=True),
    )
    device_count = all_logs.shape[0]
    own_index = lax.axis_index("ctx")
    order_index = jnp.arange(device_count)
    between = (order_index[:, None] < order_index[None, :]) & (order_index[None, :] < own_index)
    span_log = jnp.einsum("jk,kgh->jgh", between.astype(jnp.float32), all_logs, precision=highest)
    weights = jnp.where((order_index < own_index)[:, None, None], jnp.exp(span_log), 0.0)
    incoming = jnp.einsum("jgh,jghpn->ghpn", weights, states, precision=highest)
    start_log = jnp.cumsum(block_log, axis=0) - block_log
    device_running = start_log[:, None] + run_tokens
    y_value = y_local + jnp.exp(device_running)[..., None] * jnp.einsum(
        "cqgn,ghpn->cqghp", c_blocks, incoming, precision=highest
    )
    y_value = y_value + head_skip_coeff.reshape(group_count, per_group)[:, :, None] * x_blocks
    group_width = per_group * P_SIZE
    gated = y_value.reshape(token_rows, group_count, group_width) * jax.nn.silu(
        input_gate_channels.astype(jnp.float32)
    ).reshape(token_rows, group_count, group_width)
    norm_scale = lax.rsqrt(jnp.mean(gated * gated, axis=2, keepdims=True) + epsilon)
    y_normed = (
        (gated * norm_scale).reshape(token_rows, -1) * gated_norm_gain.astype(jnp.float32)
    ).astype(jnp.bfloat16)
    own_index = lax.axis_index("ctx")
    slot_count = TURN_DEV + 1
    slot_turns = TURN_DEV * own_index - 1 + jnp.arange(slot_count)
    clipped = jnp.maximum(slot_turns, 0)
    tenants = jnp.take(tenant_of_turn, clipped)
    slot_homes = jnp.take(tenant_panel_index, tenants)
    all_down, all_up = (
        lax.all_gather(adapter_down_panels, "ctx", axis=0, tiled=True),
        lax.all_gather(adapter_up_panels, "ctx", axis=0, tiled=True),
    )
    down_slots = jnp.take(all_down, slot_homes, axis=0)
    up_slots = jnp.take(all_up, slot_homes, axis=0)
    base_out = lax.psum_scatter(
        jnp.dot(y_normed, output_weight, preferred_element_type=jnp.float32).astype(jnp.bfloat16),
        "head",
        scatter_dimension=1,
        tiled=True,
    ).astype(jnp.float32)
    own_starts = lax.dynamic_slice_in_dim(turn_first_token, TURN_DEV * own_index, TURN_DEV, 0)
    token_place = own_index * token_rows + jnp.arange(token_rows)
    token_slot = jnp.sum((token_place[:, None] >= own_starts[None, :]).astype(jnp.int32), axis=1)
    slot_mask = (token_slot[:, None] == jnp.arange(slot_count)[None, :]).astype(jnp.float32)
    low_slots = jnp.einsum("tc,scr->tsr", y_normed, down_slots, preferred_element_type=jnp.float32)
    rank_reduced = jnp.sum(low_slots * slot_mask[:, :, None], axis=1)
    rank_reduced = lax.psum(rank_reduced, "head").astype(jnp.bfloat16)
    adapter_out = jnp.einsum(
        "tr,srd->tsd", rank_reduced, up_slots, preferred_element_type=jnp.float32
    )
    adapter_out = jnp.sum(adapter_out * slot_mask[:, :, None], axis=1)
    return (base_out + adapter_out).astype(jnp.bfloat16)


def solution(mesh):
    in_specs = (
        P("ctx", "head"),
        P("ctx", "head"),
        P("ctx", "head"),
        P("ctx", "head"),
        P("head", "ctx"),
        P("head"),
        P("head"),
        P(None, "head"),
        P(None, "head"),
        P(None, "head"),
        P("head"),
        P("head", None),
        P("ctx", "head", None),
        P("ctx", None, "head"),
        P(),
        P(),
        P(),
    )
    out_specs = P("ctx", "head")
    return jax.shard_map(local, mesh=mesh, in_specs=in_specs, out_specs=out_specs, check_vma=False)
```

profile of v0, /device:TPU:0, one launch (start us, length us, event | category | flops | bytes accessed | tf_op | source)
XLA Modules:
  0.0 349.8 jit_solution(5705735439827553091)
XLA Ops:
  8.2 3.9 %collective-permute-start = (bf16[3,1024]{0,1:T(8,128)(2,1)}, bf16[3,1024]{0,1:T(8,128)(2,1)S(1)}, u32[]{:S(2)}, u32[]{:S(2)}) collective-permute-start(bf16[3,1024]{0,1:T(8,128)(2,1)} %copy.74), channel_id=1, source_target_pairs={{0,8},{8,16},{16,24},{24,32},{32,40},{40,48},{48,56},{56,64},{64,7... | collective-permute-start | bytes 18440 | tf_op jit(solution)/shard_map/ppermute | solution.py:18
  12.8 3.8 %collective-permute-start.2 = (bf16[3,128]{1,0:T(4,128)(2,1)S(1)}, bf16[3,128]{1,0:T(4,128)(2,1)S(1)}, u32[]{:S(2)}, u32[]{:S(2)}) collective-permute-start(bf16[3,128]{1,0:T(4,128)(2,1)S(1)} %slice.104), channel_id=1, source_target_pairs={{0,8},{8,16},{16,24},{24,32},{32,40},{40,48},{48,56},{56,64},{64,7... | collective-permute-start | bytes 2312 | tf_op jit(solution)/shard_map/ppermute | solution.py:18
  19.1 4.5 %reduce_window_sum.22 = f32[16,8,128]{2,1,0:T(8,128)S(1)} reduce-window(f32[16,8,128]{2,1,0:T(8,128)S(1)} %negate_multiply_fusion, f32[]{:T(128)} %constant.95.clone.1), window={size=1x1x128 pad=0_0x0_0x127_0}, to_apply=%region_0.1 | reduce-window | flops 2080768 | bytes 131076 | tf_op jit(solution)/shard_map/jit(cumsum)/reduce_window_sum | solution.py:70
  29.7 5.5 %convert_bitcast_fusion = (f32[128,8,8,128]{3,1,2,0:T(8,128)}, bf16[1024,1024]{0,1:T(8,128)(2,1)S(1)}) fusion(f32[1027,1024]{0,1:T(8,128)S(1)} %maximum_convert_fusion, f32[1024]{0:T(1024)S(1)} %bitcast.186, f32[1024]{0:T(1024)S(1)} %bitcast.187, f32[1024]{0:T(1024)S(1)} %bitcast.185, f32[1024]{0:T(1024)S(1)} %bitcast.184), kind=kLoop, calls=%fused_computation.43 | loop fusion | flops 13631488 | bytes 23085056
  36.2 3.8 %fusion.31 = f32[8,1,16,64,128]{4,3,2,1,0:T(8,128)} fusion(bf16[8,128,128,1]{2,1,3,0:T(8,128)(2,1)S(1)} %bitcast.173, f32[8,128,16,64]{1,0,3,2:T(8,128)S(1)} %convert_multiply_fusion.1), kind=kOutput, calls=%fused_computation.55 | convolution fusion | flops 1610612736 | bytes 8650752 | tf_op jit(solution)/shard_map/cghk,ckghp,ckgn->cghpn/dot_general | solution.py:83
  40.0 16.3 %while.13 = (s32[]{:T(128)}, f32[1,16,64,128]{3,2,1,0:T(8,128)S(1)}, f32[8,1,16,64,128]{4,3,2,1,0:T(8,128)}, f32[8,1,16]{2,1,0:T(1,128)S(1)}, f32[8,1,16,64,128]{4,3,2,1,0:T(8,128)}, /*index=5*/s32[]{:T(128)}, s32[]{:T(128)}) while((s32[]{:T(128)}, f32[1,16,64,128]{3,2,1,0:T(8,128)S(1)}, f32[8,1,16,64,128]{4,3,2,1,0:T(8,128)}, ...), condition=%wide.region_2.3_spmd.clone, body=%wide.region_1.2_spmd.clone.sunk | while | flops 524291 | bytes 2622240 | solution.py:93
  58.7 3.5 %collective-permute-start.1 = (bf16[3,128]{1,0:T(4,128)(2,1)S(1)}, bf16[3,128]{1,0:T(4,128)(2,1)S(1)}, u32[]{:S(2)}, u32[]{:S(2)}) collective-permute-start(bf16[3,128]{1,0:T(4,128)(2,1)S(1)} %slice.95), channel_id=1, source_target_pairs={{0,8},{8,16},{16,24},{24,32},{32,40},{40,48},{48,56},{56,64},{64,7... | collective-permute-start | bytes 2312 | tf_op jit(solution)/shard_map/ppermute | solution.py:18
  63.9 36.2 %all-reduce = f32[256]{0:T(256)S(1)} all-reduce(f32[256]{0:T(256)S(1)} %dynamic-update-slice), channel_id=2, replica_groups=mesh['ctx'=16,'head'=8] {'ctx'}, use_global_device_ids=true, to_apply=%add | all-reduce | flops 256 | bytes 2048
  100.7 4.0 %copy.92 = bf16[1024,1024]{0,1:T(8,128)(2,1)} copy(bf16[1024,1024]{1,0:T(8,128)(2,1)} %param.22) | data formatting | bytes 4194304 | tf_op args[3]
  106.9 3.0 copy.104
  110.1 3.5 %fusion.21 = f32[8,16,64,128]{3,2,1,0:T(8,128)} fusion(bf16[8,128,128,1]{2,1,3,0:T(8,128)(2,1)S(1)} %bitcast.170, f32[8,1,16,64,128]{4,3,2,1,0:T(8,128)S(1)} %copy-done.8), kind=kOutput, calls=%fused_computation.38 | convolution fusion | flops 1610612736 | bytes 8650752 | tf_op jit(solution)/shard_map/cqgn,cghpn->cqghp/dot_general | solution.py:96
  113.6 11.3 %fusion.4 = f32[8,16,64,128]{3,2,1,0:T(8,128)} fusion(f32[8,16,128]{2,1,0:T(8,128)S(1)} %copy.78, f32[8,16,128]{2,1,0:T(8,128)S(1)} %copy.76, f32[8,128,128]{2,1,0:T(8,128)S(1)} %fusion.61, pred[128,128]{1,0:T(8,128)(4,1)S(1)} %iota_compare_fusion, bf16[8,128,16,64]{1,0,3,2:T(8,128)(2,1)S(1)} %bitcast.167), kind=kOutput, calls=%fused_computation.11 | convolution fusion | flops 1621098496 | bytes 6963200 | tf_op jit(solution)/shard_map/cghqk,ckghp->cqghp/dot_general | solution.py:81
  124.9 3.8 %all-gather.10.cloned.1.call-done = f32[16,16,64,128]{3,2,1,0:T(8,128)} async-done(((f32[1,16,64,128]{3,2,1,0:T(8,128)}), f32[16,16,64,128]{3,2,1,0:T(8,128)}) %all-gather.10.cloned.1.call-update) | async-done | bytes 8388624 | tf_op jit(solution)/shard_map/all_gather | solution.py:101
  128.7 12.8 %fusion.2 = f32[16,1,64,128]{3,1,2,0:T(1,128)S(1)} fusion(f32[16,16,1,1]{0,2,3,1:T(1,128)S(1)} %copy.96, f32[16,16,64,128]{3,2,1,0:T(8,128)} %all-gather.10.cloned.1.call-done), kind=kOutput, calls=%fused_computation.9 | convolution fusion | flops 25165824 | bytes 8913920 | tf_op jit(solution)/shard_map/jgh,jghpn->ghpn/dot_general | solution.py:109
  141.5 5.1 %fusion.19 = f32[8,128,1,16,64]{1,4,3,0,2:T(8,128)S(1)} fusion(f32[8,16,64,128]{3,2,1,0:T(8,128)S(1)} %copy-done.6, f32[8,16,64,128]{3,2,1,0:T(8,128)} %fusion.4, f32[8,128,1,16,64]{1,0,4,3,2:T(8,128)S(1)} %bitcast.164, f32[16,64,128,1]{2,1,0,3:T(8,128)S(1)} %bitcast.175, bf16[8,128,128,1]{2,1,3,0:T(8,128)(2,1)S(1)} %bitcast.171, f32[16]{0:T(128)S(1)} %copy-done.13, ...), kind=kOutput, calls=%fused_computation.35 | convolution fusion | flops 1616904192 | bytes 17694784 | tf_op jit(solution)/shard_map/cqgn,ghpn->cqghp/dot_general | solution.py:112
  146.6 3.3 copy.91
  153.8 11.5 %convolution_convert_fusion = bf16[1024,4096]{1,0:T(8,128)(2,1)} fusion(bf16[1024,4096]{1,0:T(8,128)(2,1)S(1)} %bitcast.189, f32[1024,1024]{0,1:T(8,128)S(1)} %get-tuple-element.84, f32[1024]{0:T(1024)S(1)} %convert_element_type.84, f32[1024]{0:T(1024)S(1)} %add_rsqrt_fusion), kind=kOutput, calls=%fused_computation.18 | convolution fusion | flops 8597274624 | bytes 20979712 | tf_op jit(solution)/shard_map/dot_general | solution.py:137
  166.9 24.9 %all-gather.8.cloned.1.call-done = bf16[96,64,512]{2,1,0:T(8,128)(2,1)} async-done(((bf16[6,64,512]{2,1,0:T(8,128)(2,1)}), bf16[96,64,512]{2,1,0:T(8,128)(2,1)}) %all-gather.8.cloned.1.call-update) | async-done | bytes 6291472 | tf_op jit(solution)/shard_map/all_gather | solution.py:132
  191.8 3.3 gather_fusion.3
  195.1 88.6 %all-gather.6.cloned.1.call-done = bf16[96,1024,64]{1,2,0:T(8,128)(2,1)} async-done(((bf16[6,1024,64]{1,2,0:T(8,128)(2,1)}), bf16[96,1024,64]{1,2,0:T(8,128)(2,1)}) %all-gather.6.cloned.1.call-update) | async-done | bytes 12582928 | tf_op jit(solution)/shard_map/all_gather | solution.py:131
  283.7 5.1 %gather_fusion.2 = bf16[3,1024,64]{1,2,0:T(8,128)(2,1)S(1)} fusion(bf16[96,1024,64]{1,2,0:T(8,128)(2,1)} %all-gather.6.cloned.1.call-done, s32[1024]{0:T(1024)S(1)} %pad_clamp_fusion), kind=kCustom, calls=%fused_computation.2 | custom fusion | bytes 786444 | tf_op jit(solution)/shard_map/jit(_take)/gather | solution.py:134
  289.0 2.9 fusion.59
  291.9 31.3 %all-reduce.2 = bf16[1024,64]{0,1:T(8,128)(2,1)S(1)} all-reduce(f32[1024,64]{0,1:T(8,128)S(1)} %multiply_reduce_fusion.2), channel_id=1, replica_groups=mesh['ctx'=16,'head'=8] {'head'}, use_global_device_ids=true, to_apply=%region_9.10 | all-reduce | flops 65536 | bytes 393216 | tf_op jit(solution)/shard_map/psum | solution.py:148
  324.3 16.4 %reduce-scatter.2.cloned.1.call-done = bf16[1024,512]{1,0:T(8,128)(2,1)} async-done(((bf16[1024,4096]{1,0:T(8,128)(2,1)}), bf16[1024,512]{1,0:T(8,128)(2,1)}) %reduce-scatter.2.cloned.1.call-update) | async-done | bytes 1048592 | tf_op jit(solution)/shard_map/reduce_scatter | solution.py:136
  (134 shorter events, 43.3 us)
Async XLA Ops:
  6.5 158.8 %copy-start = (s32[32]{0:T(128)S(1)}, s32[32]{0:T(128)}, u32[]{:S(2)}) copy-start(s32[32]{0:T(128)} %param.34) | copy-start | bytes 388
  6.5 21.5 %copy-start.9 = (bf16[1024,128]{1,0:T(8,128)(2,1)S(1)}, bf16[1024,128]{1,0:T(8,128)(2,1)}, u32[]{:S(2)}) copy-start(bf16[1024,128]{1,0:T(8,128)(2,1)} %param.20) | copy-start | bytes 786436
  6.5 122.1 %all-gather.10.cloned.1.call-start = ((), (), s32[]{:S(2)}) async-start(), calls=%async_computation.4 | async-start | bytes 8912896 | tf_op jit(solution)/shard_map/all_gather | solution.py:101
  8.2 20.3 %collective-permute-start = (bf16[3,1024]{0,1:T(8,128)(2,1)}, bf16[3,1024]{0,1:T(8,128)(2,1)S(1)}, u32[]{:S(2)}, u32[]{:S(2)}) collective-permute-start(bf16[3,1024]{0,1:T(8,128)(2,1)} %copy.74), channel_id=1, source_target_pairs={{0,8},{8,16},{16,24},{24,32},{32,40},{40,48},{48,56},{56,64},{64,7... | collective-permute-start | bytes 18440 | tf_op jit(solution)/shard_map/ppermute | solution.py:18
  12.8 15.2 %collective-permute-start.2 = (bf16[3,128]{1,0:T(4,128)(2,1)S(1)}, bf16[3,128]{1,0:T(4,128)(2,1)S(1)}, u32[]{:S(2)}, u32[]{:S(2)}) collective-permute-start(bf16[3,128]{1,0:T(4,128)(2,1)S(1)} %slice.104), channel_id=1, source_target_pairs={{0,8},{8,16},{16,24},{24,32},{32,40},{40,48},{48,56},{56,64},{64,7... | collective-permute-start | bytes 2312 | tf_op jit(solution)/shard_map/ppermute | solution.py:18
  40.0 18.7 %copy-start.10 = (bf16[1024,128]{1,0:T(8,128)(2,1)S(1)}, bf16[1024,128]{1,0:T(8,128)(2,1)}, u32[]{:S(2)}) copy-start(bf16[1024,128]{1,0:T(8,128)(2,1)} %param.21) | copy-start | bytes 786436
  40.0 22.2 %copy-start.15 = (u32[128]{0:T(128)S(1)}, u32[128]{0:T(128)}, u32[]{:S(2)}) copy-start(u32[128]{0:T(128)} %constant.114) | copy-start | bytes 1540
  40.0 60.3 %copy-start.11 = (bf16[4,128]{1,0:T(4,128)(2,1)S(1)}, bf16[4,128]{1,0:T(4,128)(2,1)}, u32[]{:S(2)}) copy-start(bf16[4,128]{1,0:T(4,128)(2,1)} %param.28) | copy-start | bytes 3076
  56.3 0.8 copy-start.2
  56.3 48.3 %copy-start.12 = (bf16[1024]{0:T(1024)(128)(2,1)S(1)}, bf16[1024]{0:T(1024)(128)(2,1)}, u32[]{:S(2)}) copy-start(bf16[1024]{0:T(1024)(128)(2,1)} %param.29) | copy-start | bytes 6148
  57.1 134.6 %all-gather.8.cloned.1.call-start = ((), (), s32[]{:S(2)}) async-start(), calls=%async_computation.3 | async-start | bytes 6684672 | tf_op jit(solution)/shard_map/all_gather | solution.py:132
  57.9 225.8 %all-gather.6.cloned.1.call-start = ((), (), s32[]{:S(2)}) async-start(), calls=%async_computation.2 | async-start | bytes 13369344 | tf_op jit(solution)/shard_map/all_gather | solution.py:131
  58.6 282.1 %reduce-scatter.2.cloned.1.call-start = ((), (), s32[]{:S(2)}) async-start(), calls=%async_computation.1 | async-start | bytes 9437184 | tf_op jit(solution)/shard_map/reduce_scatter | solution.py:136
  58.7 46.0 %collective-permute-start.1 = (bf16[3,128]{1,0:T(4,128)(2,1)S(1)}, bf16[3,128]{1,0:T(4,128)(2,1)S(1)}, u32[]{:S(2)}, u32[]{:S(2)}) collective-permute-start(bf16[3,128]{1,0:T(4,128)(2,1)S(1)} %slice.95), channel_id=1, source_target_pairs={{0,8},{8,16},{16,24},{24,32},{32,40},{40,48},{48,56},{56,64},{64,7... | collective-permute-start | bytes 2312 | tf_op jit(solution)/shard_map/ppermute | solution.py:18
  104.6 2.2 copy-start.3
  106.9 3.2 copy-start.8
  124.9 16.7 %copy-start.13 = (f32[16]{0:T(128)S(1)}, f32[16]{0:T(128)}, u32[]{:S(2)}) copy-start(f32[16]{0:T(128)} %param.25) | copy-start | bytes 196
  128.7 12.9 %copy-start.5 = (f32[128,8,8,128]{3,2,1,0:T(8,128)S(1)}, f32[128,8,8,128]{3,2,1,0:T(8,128)}, u32[]{:S(2)}) copy-start(f32[128,8,8,128]{3,2,1,0:T(8,128)} %copy.104) | copy-start | bytes 12582916
  128.7 12.9 %copy-start.6 = (f32[8,16,64,128]{3,2,1,0:T(8,128)S(1)}, f32[8,16,64,128]{3,2,1,0:T(8,128)}, u32[]{:S(2)}) copy-start(f32[8,16,64,128]{3,2,1,0:T(8,128)} %fusion.21) | copy-start | bytes 12582916
  146.6 3.3 copy-start.7
  146.6 7.2 %slice-start = ((s8[8388608]{0:T(1024)(128)(4,1)}), s8[4194304]{0:T(1024)(128)(4,1)S(1)}, s32[]{:S(2)}) async-start(s8[8388608]{0:T(1024)(128)(4,1)} %bitcast.188), calls=%async_computation.5 | async-start | bytes 8388608
  150.0 3.8 %slice-start.1 = ((s8[8388608]{0:T(1024)(128)(4,1)}), s8[4194304]{0:T(1024)(128)(4,1)S(1)}, s32[]{:S(2)}) async-start(s8[8388608]{0:T(1024)(128)(4,1)} %bitcast.188), calls=%async_computation.6 | async-start | bytes 8388608
  151.7 2.0 copy-start.4
  165.3 1.4 copy-start.14
  (1 other events, 0.7 us)
Sparse Core Ops, SparseCore 0:
  57.3 71.3 all-gather.9
  130.8 60.8 all-gather.7
  194.0 89.7 all-gather.5
  286.0 54.6 reduce-scatter.1
where the time goes:
time: 351 us; the launch traced here: 350 us
  waiting for transfers between devices  135 us (38%)
  blocking collectives  67.5 us (19%)
  matrix products  52.3 us (15%)
  other arithmetic  36.4 us (10%)
  local copies, waits for them, and re-layouts  32.7 us (9%)
  between operations  14.3 us (4%)
  starting transfers between devices  11.4 us (3%)
    all_gather x1, waiting for transfers between devices, local(): lax.all_gather(adapter_down_panels, 'ctx', axis=0, tiled=True)  88.6 us
    unnamed x1, blocking collectives  36.2 us
    psum x1, blocking collectives, local(): rank_reduced = lax.psum(rank_reduced, 'head').astype(jnp.bfloat16)  31.3 us
    all_gather x1, waiting for transfers between devices, local(): lax.all_gather(adapter_up_panels, 'ctx', axis=0, tiled=True)  24.9 us
    reduce_scatter x1, waiting for transfers between devices, local(): lax.psum_scatter(jnp.dot(y_normed, output_weight, preferred_element_type=...  16.4 us
    unnamed x44, local copies, waits for them, and re-layouts  15.9 us
    dot_general x1, matrix products, local(): incoming = jnp.einsum('jgh,jghpn->ghpn', weights, states, precision=highest)  12.8 us
    dot_general x1, matrix products, local(): jnp.dot(y_normed, output_weight, preferred_element_type=jnp.float32)  11.5 us
  transfers between devices with their start and end apart: 7, of which 4 were waited for; matrix products, arithmetic and copies ran while one was open for 24% of the time, Pallas kernels for 0%

commit v1 on v0

--- a/solution.py
+++ b/solution.py
@@ -10,6 +10,12 @@
 TURN_DEV = 2
 highest = lax.Precision.HIGHEST
 epsilon = 1e-05
+
+
+def gather_by_exchange(x, axis, dim):
+    size = lax.axis_size(axis)
+    repeats = [size if d == dim else 1 for d in range(x.ndim)]
+    return lax.all_to_all(jnp.tile(x, repeats), axis, split_axis=dim, concat_axis=dim, tiled=True)
 
 
 def shifted(block, axis, distance):
@@ -129,7 +135,7 @@
     slot_homes = jnp.take(tenant_panel_index, tenants)
     all_down, all_up = (
         lax.all_gather(adapter_down_panels, "ctx", axis=0, tiled=True),
-        lax.all_gather(adapter_up_panels, "ctx", axis=0, tiled=True),
+        gather_by_exchange(adapter_up_panels, "ctx", 0),
     )
     down_slots = jnp.take(all_down, slot_homes, axis=0)
     up_slots = jnp.take(all_up, slot_homes, axis=0)

time: 351 us -> 367 us (1.046)
  starting transfers between devices: 11.4 us -> 17.3 us
  local copies, waits for them, and re-layouts: 32.7 us -> 37.7 us
    all_to_all x0 -> x1, waiting for transfers between devices: none -> 128 us  [gather_by_exchange(): lax.all_to_all(jnp.tile(x, repeats), axis, split_axis=dim, concat_axis=di...]
    all_gather x1, waiting for transfers between devices: 88.6 us -> 0.02 us  [local(): lax.all_gather(adapter_down_panels, 'ctx', axis=0, tiled=True)]
    all_gather x1 -> x0, waiting for transfers between devices: 24.9 us -> none  [local(): lax.all_gather(adapter_up_panels, 'ctx', axis=0, tiled=True)]
    reduce_scatter x1, waiting for transfers between devices: 16.4 us -> 0.02 us  [local(): lax.psum_scatter(jnp.dot(y_normed, output_weight, preferred_element_type=...]
    all_to_all x0 -> x1, starting transfers between devices: none -> 5.94 us  [gather_by_exchange(): lax.all_to_all(jnp.tile(x, repeats), axis, split_axis=dim, concat_axis=di...]
    unnamed x44 -> x54, local copies, waits for them, and re-layouts: 15.9 us -> 17.3 us
  transfers between devices with their start and end apart: 7 -> 7, of which waited for: 4 -> 2; matrix products, arithmetic and copies ran while one was open for 24% -> 25% of each run, Pallas kernels for 0% -> 0%
where the time goes in v1:
time: 367 us; the launch traced here: 363 us
  waiting for transfers between devices  134 us (37%)
  blocking collectives  67.6 us (18%)
  matrix products  52.6 us (14%)
  other arithmetic  39.6 us (11%)
  local copies, waits for them, and re-layouts  37.7 us (10%)
  starting transfers between devices  17.3 us (5%)
  between operations  14.3 us (4%)
    all_to_all x1, waiting for transfers between devices, gather_by_exchange(): lax.all_to_all(jnp.tile(x, repeats), axis, split_axis=dim, concat_axis=di...  128 us
    unnamed x1, blocking collectives  36.2 us
    psum x1, blocking collectives, local(): rank_reduced = lax.psum(rank_reduced, 'head').astype(jnp.bfloat16)  31.4 us
    unnamed x54, local copies, waits for them, and re-layouts  17.3 us
    dot_general x1, matrix products, local(): incoming = jnp.einsum('jgh,jghpn->ghpn', weights, states, precision=highest)  12.8 us
    dot_general x1, matrix products, local(): jnp.dot(y_normed, output_weight, preferred_element_type=jnp.float32)  11.5 us
    dot_general x1, matrix products, local(): jnp.einsum('cghqk,ckghp->cqghp', mixing, x_blocks, precision=highest)  11.3 us
    ppermute x3, starting transfers between devices, shifted(): return lax.ppermute(block, axis, route)  11.2 us
  transfers between devices with their start and end apart: 7, of which 2 were waited for; matrix products, arithmetic and copies ran while one was open for 25% of the time, Pallas kernels for 0%

profile of v1, /device:TPU:0, one launch (start us, length us, event | category | flops | bytes accessed | tf_op | source)
XLA Modules:
  0.0 362.9 jit_solution(10238147997212758289)
XLA Ops:
  8.2 3.9 %collective-permute-start = (bf16[3,1024]{0,1:T(8,128)(2,1)}, bf16[3,1024]{0,1:T(8,128)(2,1)S(1)}, u32[]{:S(2)}, u32[]{:S(2)}) collective-permute-start(bf16[3,1024]{0,1:T(8,128)(2,1)} %copy.74), channel_id=1, source_target_pairs={{0,8},{8,16},{16,24},{24,32},{32,40},{40,48},{48,56},{56,64},{64,7... | collective-permute-start | bytes 18440 | tf_op jit(solution)/shard_map/ppermute | solution.py:24
  12.8 3.8 %collective-permute-start.2 = (bf16[3,128]{1,0:T(4,128)(2,1)S(1)}, bf16[3,128]{1,0:T(4,128)(2,1)S(1)}, u32[]{:S(2)}, u32[]{:S(2)}) collective-permute-start(bf16[3,128]{1,0:T(4,128)(2,1)S(1)} %slice.104), channel_id=1, source_target_pairs={{0,8},{8,16},{16,24},{24,32},{32,40},{40,48},{48,56},{56,64},{64,7... | collective-permute-start | bytes 2312 | tf_op jit(solution)/shard_map/ppermute | solution.py:24
  19.7 4.5 %reduce_window_sum.22 = f32[16,8,128]{2,1,0:T(8,128)S(1)} reduce-window(f32[16,8,128]{2,1,0:T(8,128)S(1)} %negate_multiply_fusion, f32[]{:T(128)} %constant.95.clone.1), window={size=1x1x128 pad=0_0x0_0x127_0}, to_apply=%region_0.1 | reduce-window | flops 2080768 | bytes 131076 | tf_op jit(solution)/shard_map/jit(cumsum)/reduce_window_sum | solution.py:76
  32.8 5.5 %convert_bitcast_fusion = (f32[128,8,8,128]{3,1,2,0:T(8,128)}, bf16[1024,1024]{0,1:T(8,128)(2,1)S(1)}) fusion(f32[1027,1024]{0,1:T(8,128)S(1)} %maximum_convert_fusion, f32[1024]{0:T(1024)S(1)} %bitcast.188, f32[1024]{0:T(1024)S(1)} %bitcast.189, f32[1024]{0:T(1024)S(1)} %bitcast.187, f32[1024]{0:T(1024)S(1)} %bitcast.186), kind=kLoop, calls=%fused_computation.43 | loop fusion | flops 13631488 | bytes 23085056
  39.6 3.8 %fusion.31 = f32[8,1,16,64,128]{4,3,2,1,0:T(8,128)} fusion(bf16[8,128,128,1]{2,1,3,0:T(8,128)(2,1)S(1)} %bitcast.175, f32[8,128,16,64]{1,0,3,2:T(8,128)S(1)} %convert_multiply_fusion.1), kind=kOutput, calls=%fused_computation.55 | convolution fusion | flops 1610612736 | bytes 8650752 | tf_op jit(solution)/shard_map/cghk,ckghp,ckgn->cghpn/dot_general | solution.py:89
  43.4 16.3 %while.13 = (s32[]{:T(128)}, f32[1,16,64,128]{3,2,1,0:T(8,128)S(1)}, f32[8,1,16,64,128]{4,3,2,1,0:T(8,128)}, f32[8,1,16]{2,1,0:T(1,128)S(1)}, f32[8,1,16,64,128]{4,3,2,1,0:T(8,128)}, /*index=5*/s32[]{:T(128)}, s32[]{:T(128)}) while((s32[]{:T(128)}, f32[1,16,64,128]{3,2,1,0:T(8,128)S(1)}, f32[8,1,16,64,128]{4,3,2,1,0:T(8,128)}, ...), condition=%wide.region_2.3_spmd.clone, body=%wide.region_1.2_spmd.clone.sunk | while | flops 524291 | bytes 2622240 | solution.py:99
  61.4 3.5 collective-permute-start.1
  66.6 36.2 %all-reduce = f32[256]{0:T(256)S(1)} all-reduce(f32[256]{0:T(256)S(1)} %dynamic-update-slice), channel_id=2, replica_groups=mesh['ctx'=16,'head'=8] {'ctx'}, use_global_device_ids=true, to_apply=%add | all-reduce | flops 256 | bytes 2048
  103.4 3.9 %copy.92 = bf16[1024,1024]{0,1:T(8,128)(2,1)} copy(bf16[1024,1024]{1,0:T(8,128)(2,1)} %param.22) | data formatting | bytes 4194304 | tf_op args[3]
  109.6 3.0 copy.104
  112.8 3.5 fusion.21
  116.3 11.3 %fusion.4 = f32[8,16,64,128]{3,2,1,0:T(8,128)} fusion(f32[8,16,128]{2,1,0:T(8,128)S(1)} %copy.78, f32[8,16,128]{2,1,0:T(8,128)S(1)} %copy.76, f32[8,128,128]{2,1,0:T(8,128)S(1)} %fusion.61, pred[128,128]{1,0:T(8,128)(4,1)S(1)} %iota_compare_fusion, bf16[8,128,16,64]{1,0,3,2:T(8,128)(2,1)S(1)} %bitcast.169), kind=kOutput, calls=%fused_computation.11 | convolution fusion | flops 1621098496 | bytes 6963200 | tf_op jit(solution)/shard_map/cghqk,ckghp->cqghp/dot_general | solution.py:87
  127.7 4.4 %all-gather.7.cloned.1.call-done = f32[16,16,64,128]{3,2,1,0:T(8,128)} async-done(((f32[1,16,64,128]{3,2,1,0:T(8,128)}), f32[16,16,64,128]{3,2,1,0:T(8,128)}) %all-gather.7.cloned.1.call-update) | async-done | bytes 8388624 | tf_op jit(solution)/shard_map/all_gather | solution.py:107
  132.1 12.8 %fusion.2 = f32[16,1,64,128]{3,1,2,0:T(1,128)S(1)} fusion(f32[16,16,1,1]{0,2,3,1:T(1,128)S(1)} %copy.96, f32[16,16,64,128]{3,2,1,0:T(8,128)} %all-gather.7.cloned.1.call-done), kind=kOutput, calls=%fused_computation.9 | convolution fusion | flops 25165824 | bytes 8913920 | tf_op jit(solution)/shard_map/jgh,jghpn->ghpn/dot_general | solution.py:115
  145.0 5.2 %fusion.19 = f32[8,128,1,16,64]{1,4,3,0,2:T(8,128)S(1)} fusion(f32[8,16,64,128]{3,2,1,0:T(8,128)S(1)} %copy-done.6, f32[8,16,64,128]{3,2,1,0:T(8,128)} %fusion.4, f32[8,128,1,16,64]{1,0,4,3,2:T(8,128)S(1)} %bitcast.166, f32[16,64,128,1]{2,1,0,3:T(8,128)S(1)} %bitcast.177, bf16[8,128,128,1]{2,1,3,0:T(8,128)(2,1)S(1)} %bitcast.173, f32[16]{0:T(128)S(1)} %copy-done.17, ...), kind=kOutput, calls=%fused_computation.35 | convolution fusion | flops 1616904192 | bytes 17694784 | tf_op jit(solution)/shard_map/cqgn,ghpn->cqghp/dot_general | solution.py:118
  150.2 3.3 copy.91
  157.4 11.5 %convolution_convert_fusion = bf16[1024,4096]{1,0:T(8,128)(2,1)} fusion(bf16[1024,4096]{1,0:T(8,128)(2,1)S(1)} %bitcast.191, f32[1024,1024]{0,1:T(8,128)S(1)} %get-tuple-element.84, f32[1024]{0:T(1024)S(1)} %convert_element_type.84, f32[1024]{0:T(1024)S(1)} %add_rsqrt_fusion), kind=kOutput, calls=%fused_computation.18 | convolution fusion | flops 8597274624 | bytes 20979712 | tf_op jit(solution)/shard_map/dot_general | solution.py:143
  169.9 3.4 tile.4
  173.3 5.9 %all-to-all-start = ((bf16[96,64,512]{2,1,0:T(8,128)(2,1)}), bf16[96,64,512]{2,1,0:T(8,128)(2,1)}, u32[]{:S(2)}, u32[]{:S(2)}) async-start(bf16[96,64,512]{2,1,0:T(8,128)(2,1)} %bitcast.165), calls=%async_computation.1 | async-start | bytes 12582912 | tf_op jit(solution)/shard_map/all_to_all | solution.py:18
  180.9 128.4 %all-to-all-done = bf16[96,64,512]{2,1,0:T(8,128)(2,1)} async-done(((bf16[96,64,512]{2,1,0:T(8,128)(2,1)}), bf16[96,64,512]{2,1,0:T(8,128)(2,1)}, u32[]{:S(2)}, u32[]{:S(2)}) %all-to-all-start) | async-done | bytes 6291488 | tf_op jit(solution)/shard_map/all_to_all | solution.py:18
  309.3 3.4 gather_fusion.3
  312.7 5.4 %gather_fusion.2 = bf16[3,1024,64]{1,2,0:T(8,128)(2,1)S(1)} fusion(bf16[96,1024,64]{1,2,0:T(8,128)(2,1)} %all-gather.5.cloned.1.call-done, s32[1024]{0:T(1024)S(1)} %pad_clamp_fusion), kind=kCustom, calls=%fused_computation.2 | custom fusion | bytes 786444 | tf_op jit(solution)/shard_map/jit(_take)/gather | solution.py:140
  318.2 2.9 fusion.59
  321.2 31.4 %all-reduce.2 = bf16[1024,64]{0,1:T(8,128)(2,1)S(1)} all-reduce(f32[1024,64]{0,1:T(8,128)S(1)} %multiply_reduce_fusion.2), channel_id=1, replica_groups=mesh['ctx'=16,'head'=8] {'head'}, use_global_device_ids=true, to_apply=%region_9.10 | all-reduce | flops 65536 | bytes 393216 | tf_op jit(solution)/shard_map/psum | solution.py:154
  (144 shorter events, 47.2 us)
Async XLA Ops:
  6.5 172.8 %copy-start = (s32[32]{0:T(128)S(1)}, s32[32]{0:T(128)}, u32[]{:S(2)}) copy-start(s32[32]{0:T(128)} %param.34) | copy-start | bytes 388
  6.5 23.9 %copy-start.10 = (bf16[1024,128]{1,0:T(8,128)(2,1)S(1)}, bf16[1024,128]{1,0:T(8,128)(2,1)}, u32[]{:S(2)}) copy-start(bf16[1024,128]{1,0:T(8,128)(2,1)} %param.20) | copy-start | bytes 786436
  6.5 125.5 %all-gather.7.cloned.1.call-start = ((), (), s32[]{:S(2)}) async-start(), calls=%async_computation.4 | async-start | bytes 8912896 | tf_op jit(solution)/shard_map/all_gather | solution.py:107
  8.2 23.3 %collective-permute-start = (bf16[3,1024]{0,1:T(8,128)(2,1)}, bf16[3,1024]{0,1:T(8,128)(2,1)S(1)}, u32[]{:S(2)}, u32[]{:S(2)}) collective-permute-start(bf16[3,1024]{0,1:T(8,128)(2,1)} %copy.74), channel_id=1, source_target_pairs={{0,8},{8,16},{16,24},{24,32},{32,40},{40,48},{48,56},{56,64},{64,7... | collective-permute-start | bytes 18440 | tf_op jit(solution)/shard_map/ppermute | solution.py:24
  12.8 17.6 %collective-permute-start.2 = (bf16[3,128]{1,0:T(4,128)(2,1)S(1)}, bf16[3,128]{1,0:T(4,128)(2,1)S(1)}, u32[]{:S(2)}, u32[]{:S(2)}) collective-permute-start(bf16[3,128]{1,0:T(4,128)(2,1)S(1)} %slice.104), channel_id=1, source_target_pairs={{0,8},{8,16},{16,24},{24,32},{32,40},{40,48},{48,56},{56,64},{64,7... | collective-permute-start | bytes 2312 | tf_op jit(solution)/shard_map/ppermute | solution.py:24
  43.4 18.0 %copy-start.11 = (bf16[1024,128]{1,0:T(8,128)(2,1)S(1)}, bf16[1024,128]{1,0:T(8,128)(2,1)}, u32[]{:S(2)}) copy-start(bf16[1024,128]{1,0:T(8,128)(2,1)} %param.21) | copy-start | bytes 786436
  43.4 21.5 %copy-start.20 = (u32[128]{0:T(128)S(1)}, u32[128]{0:T(128)}, u32[]{:S(2)}) copy-start(u32[128]{0:T(128)} %constant.114) | copy-start | bytes 1540
  43.4 22.9 %copy-start.18 = (f32[16]{0:T(128)S(1)}, f32[16]{0:T(128)}, u32[]{:S(2)}) copy-start(f32[16]{0:T(128)} %get-tuple-element.89) | copy-start | bytes 196
  43.4 59.7 %copy-start.15 = (bf16[4,128]{1,0:T(4,128)(2,1)S(1)}, bf16[4,128]{1,0:T(4,128)(2,1)}, u32[]{:S(2)}) copy-start(bf16[4,128]{1,0:T(4,128)(2,1)} %param.28) | copy-start | bytes 3076
  59.8 47.5 %copy-start.16 = (bf16[1024]{0:T(1024)(128)(2,1)S(1)}, bf16[1024]{0:T(1024)(128)(2,1)}, u32[]{:S(2)}) copy-start(bf16[1024]{0:T(1024)(128)(2,1)} %param.29) | copy-start | bytes 6148
  60.6 252.1 %all-gather.5.cloned.1.call-start = ((), (), s32[]{:S(2)}) async-start(), calls=%async_computation.3 | async-start | bytes 13369344 | tf_op jit(solution)/shard_map/all_gather | solution.py:137
  61.3 292.4 %reduce-scatter.2.cloned.1.call-start = ((), (), s32[]{:S(2)}) async-start(), calls=%async_computation.2 | async-start | bytes 9437184 | tf_op jit(solution)/shard_map/reduce_scatter | solution.py:142
  61.4 45.9 %collective-permute-start.1 = (bf16[3,128]{1,0:T(4,128)(2,1)S(1)}, bf16[3,128]{1,0:T(4,128)(2,1)S(1)}, u32[]{:S(2)}, u32[]{:S(2)}) collective-permute-start(bf16[3,128]{1,0:T(4,128)(2,1)S(1)} %slice.95), channel_id=1, source_target_pairs={{0,8},{8,16},{16,24},{24,32},{32,40},{40,48},{48,56},{56,64},{64,7... | collective-permute-start | bytes 2312 | tf_op jit(solution)/shard_map/ppermute | solution.py:24
  107.3 2.3 copy-start.3
  109.6 3.2 copy-start.8
  127.7 17.3 %copy-start.17 = (f32[16]{0:T(128)S(1)}, f32[16]{0:T(128)}, u32[]{:S(2)}) copy-start(f32[16]{0:T(128)} %param.25) | copy-start | bytes 196
  132.1 12.9 %copy-start.5 = (f32[128,8,8,128]{3,2,1,0:T(8,128)S(1)}, f32[128,8,8,128]{3,2,1,0:T(8,128)}, u32[]{:S(2)}) copy-start(f32[128,8,8,128]{3,2,1,0:T(8,128)} %copy.104) | copy-start | bytes 12582916
  132.1 12.9 %copy-start.6 = (f32[8,16,64,128]{3,2,1,0:T(8,128)S(1)}, f32[8,16,64,128]{3,2,1,0:T(8,128)}, u32[]{:S(2)}) copy-start(f32[8,16,64,128]{3,2,1,0:T(8,128)} %fusion.21) | copy-start | bytes 12582916
  150.2 3.4 copy-start.7
  150.2 7.2 %slice-start = ((s8[8388608]{0:T(1024)(128)(4,1)}), s8[4194304]{0:T(1024)(128)(4,1)S(1)}, s32[]{:S(2)}) async-start(s8[8388608]{0:T(1024)(128)(4,1)} %bitcast.190), calls=%async_computation.5 | async-start | bytes 8388608
  153.5 3.8 %slice-start.1 = ((s8[8388608]{0:T(1024)(128)(4,1)}), s8[4194304]{0:T(1024)(128)(4,1)S(1)}, s32[]{:S(2)}) async-start(s8[8388608]{0:T(1024)(128)(4,1)} %bitcast.190), calls=%async_computation.6 | async-start | bytes 8388608
  173.3 6.7 %copy-start.1 = (s32[96]{0:T(128)S(1)}, s32[96]{0:T(128)}, u32[]{:S(2)}) copy-start(s32[96]{0:T(128)} %param.35) | copy-start | bytes 1156
  173.3 7.3 %copy-start.19 = (s32[32]{0:T(128)S(1)}, s32[32]{0:T(128)}, u32[]{:S(2)}) copy-start(s32[32]{0:T(128)} %param.33) | copy-start | bytes 388
  173.3 136.0 %all-to-all-start = ((bf16[96,64,512]{2,1,0:T(8,128)(2,1)}), bf16[96,64,512]{2,1,0:T(8,128)(2,1)}, u32[]{:S(2)}, u32[]{:S(2)}) async-start(bf16[96,64,512]{2,1,0:T(8,128)(2,1)} %bitcast.165), calls=%async_computation.1 | async-start | bytes 12582912 | tf_op jit(solution)/shard_map/all_to_all | solution.py:18
  (6 other events, 9.4 us)
Sparse Core Ops, SparseCore 0:
  60.7 71.3 all-gather.6
  134.3 157.6 all-gather.4
  294.4 57.7 reduce-scatter.1
